TPU v7x, 32 devices: a whole 2x2x4 slice. The times are simulated.
32 devices in a mesh: dev: 8 (over z, x), rep: 4 (over y, core).
Axes of the slice: x: 2, y: 2, z: 4, core: 2. Of those that a mesh axis runs over, the one named last changes fastest.
Arguments:
- h_zero: bfloat16 [32768, 256], P(('dev', 'rep')), may hold values from 0 to 2
- h_prev: bfloat16 [32768, 256], P(('dev', 'rep')), may hold values from 0 to 2
- hist_a: bfloat16 [32768, 256], P('dev'), may hold values from 0 to 2
- hist_b: bfloat16 [32768, 256], P('dev'), may hold values from 0 to 2
- tile_vals: bfloat16 [256, 12, 128, 128], P(('dev', 'rep'))
- tile_cols: int32 [256, 12], P(('dev', 'rep')), may hold values from 0 to 47, as said below
- pull_rows: int32 [32, 8, 128], P(('dev', 'rep')), may hold values from 0 to 4095
- pull_counts: int32 [32, 8], P(('dev', 'rep')), may hold values from 96 to 128, as said below
- weight_two: bfloat16 [256, 256], replicated, may hold values from -0.375 to 0.375
- weight_three: bfloat16 [256, 256], replicated, may hold values from -0.375 to 0.375
- grad_out: bfloat16 [32768, 256], P(('dev', 'rep')), may hold values from -0.125 to 0.125
Outputs:
- layer_three: bfloat16 [32768, 256], P(('dev', 'rep'))
- new_history: bfloat16 [32768, 256], P('dev')
- weight_grad: float32 [256, 256], replicated
Inputs may be any that keep to these rules, and one draw needn't show every extreme that they name: `tile_cols`: entry 0 of a row block names one of its device's own 8 blocks; entries 1 to 3 name blocks of the owner's history shard; the other 8 name pulled blocks of consecutive owners modulo 8, and every owner's block is named by some row block of each device. `pull_rows`: entries at slots at or past the block's count are read by no output. `pull_counts`: every device pulls a full block of 128 rows from some owner and a block of exactly 96 rows from another.
All inputs are finite; a program needn't handle non-finite values.
Results may differ from a plain program's by a relative error of at most 0.0034.
Values may be sent and summed in bfloat16 or wider, within the bound.
No kernel may reach another device: no remote copies, remote signals or barrier semaphores. Data moves between devices by JAX's collectives and lax.ppermute only.
A program may use at most 128 MiB of HBM per device.

v0:
```python
import math
import jax
import jax.numpy as jnp
from jax import lax
from jax.sharding import PartitionSpec as P

restart = 0.1
strength = 0.5


def propagate(current, history, pulled, values, columns, start_rows, weight, layer_number):
    feature_width = current.shape[1]
    tile_size = values.shape[2]
    source = jnp.concatenate([current, history, pulled.reshape(-1, feature_width)], axis=0)
    blocks = source.reshape(-1, tile_size, feature_width)
    picked = jnp.take(blocks, columns.reshape(-1), axis=0).reshape(
        columns.shape + (tile_size, feature_width)
    )
    summed = jnp.einsum("btij,btjf->bif", values, picked, preferred_element_type=jnp.float32)
    summed = summed.reshape(current.shape[0], feature_width)
    mixed_rows = (1.0 - restart) * summed + restart * start_rows.astype(jnp.float32)
    mixed_low = mixed_rows.astype(jnp.bfloat16)
    factor = math.log(strength / layer_number + 1.0)
    product = jnp.dot(mixed_low, weight, preferred_element_type=jnp.float32)
    inner_sum = (1.0 - factor) * mixed_rows + factor * product
    return (jnp.maximum(inner_sum, 0.0).astype(jnp.bfloat16), mixed_low)


def local(
    h_zero,
    h_prev,
    hist_a,
    hist_b,
    tile_vals,
    tile_cols,
    pull_rows,
    pull_counts,
    weight_two,
    weight_three,
    grad_out,
):
    wanted = pull_rows[0]
    peer_count, slot_count = wanted.shape
    feature_width = hist_a.shape[1]
    asked_rows = lax.all_to_all(wanted, "dev", split_axis=0, concat_axis=0, tiled=True)
    flat_rows = asked_rows.reshape(-1)
    live_mask = (lax.broadcasted_iota(jnp.int32, wanted.shape, 1) < pull_counts[0][:, None])[
        :, :, None
    ]

    def serve_rows(history):
        return jnp.take(history, flat_rows, axis=0).reshape(peer_count, slot_count, feature_width)

    def trim_rows(arrived):
        return jnp.where(live_mask, arrived, jnp.zeros((), jnp.bfloat16))

    reply_a = lax.all_to_all(serve_rows(hist_a), "dev", split_axis=0, concat_axis=0, tiled=True)
    second, unused_mix = propagate(
        h_prev, hist_a, trim_rows(reply_a), tile_vals, tile_cols, h_zero, weight_two, 2
    )
    reply_b = lax.all_to_all(serve_rows(hist_b), "dev", split_axis=0, concat_axis=0, tiled=True)
    fresh_rows = lax.all_gather(second, "rep", axis=0, tiled=True)
    layer_three, mixed_low = propagate(
        second, hist_b, trim_rows(reply_b), tile_vals, tile_cols, h_zero, weight_three, 3
    )
    factor = math.log(strength / 3 + 1.0)
    grad_term = factor * lax.dot_general(
        mixed_low, grad_out, (((0,), (0,)), ((), ())), preferred_element_type=jnp.float32
    )
    grad_total = lax.psum(grad_term, ("dev", "rep"))
    return (layer_three, fresh_rows, grad_total)


def solution(mesh):
    return jax.shard_map(
        local,
        mesh=mesh,
        in_specs=(
            P(("dev", "rep"), None),
            P(("dev", "rep"), None),
            P("dev", None),
            P("dev", None),
            P(("dev", "rep"), None, None, None),
            P(("dev", "rep"), None),
            P(("dev", "rep"), None, None),
            P(("dev", "rep"), None),
            P(),
            P(),
            P(("dev", "rep"), None),
        ),
        out_specs=(P(("dev", "rep"), None), P("dev", None), P()),
        check_vma=False,
    )
```

profile of v0, /device:TPU:0, one launch (start us, length us, event | category | flops | bytes accessed | tf_op | source)
XLA Modules:
  0.0 246.1 jit_solution(17458504703795671243)
XLA Ops:
  8.0 0.0 copy-start
  8.0 14.0 %all_to_all.19 = s32[8,1,128]{2,1,0:T(1,128)S(1)} all-to-all(s32[8,1,128]{2,1,0:T(1,128)} %bitcast.46), channel_id=1, replica_groups=mesh['dev'=8,'rep'=4] {'dev'}, dimensions={0} | all-to-all | bytes 8192 | tf_op jit(solution)/shard_map/all_to_all | solution.py:45
  22.0 0.0 copy-start.7
  22.0 0.0 copy-start.8
  22.0 6.5 %gather_fusion = bf16[1024,256]{1,0:T(8,128)(2,1)} fusion(bf16[4096,256]{1,0:T(8,128)(2,1)} %param.17, s32[1024]{0:T(1024)S(1)} %fusion.11), kind=kCustom, calls=%fused_computation.clone | custom fusion | bytes 1052672 | tf_op jit(solution)/shard_map/jit(_take)/gather | solution.py:52
  28.5 6.5 %gather_fusion.2 = bf16[1024,256]{1,0:T(8,128)(2,1)} fusion(bf16[4096,256]{1,0:T(8,128)(2,1)} %param.18, s32[1024]{0:T(1024)S(1)} %fusion.11), kind=kCustom, calls=%fused_computation.2.clone | custom fusion | bytes 1052672 | tf_op jit(solution)/shard_map/jit(_take)/gather | solution.py:52
  35.0 2.2 broadcast_select_fusion.3
  37.2 16.4 %all_to_all.20 = bf16[8,128,256]{2,1,0:T(8,128)(2,1)} all-to-all(bf16[8,128,256]{2,1,0:T(8,128)(2,1)S(1)} %bitcast.43), channel_id=1, replica_groups=mesh['dev'=8,'rep'=4] {'dev'}, dimensions={0} | all-to-all | bytes 1048576 | tf_op jit(solution)/shard_map/all_to_all | solution.py:57
  53.6 4.1 %all-to-all-start.2 = ((bf16[8,128,256]{2,1,0:T(8,128)(2,1)}), bf16[8,128,256]{2,1,0:T(8,128)(2,1)}, u32[]{:S(2)}, u32[]{:S(2)}) async-start(bf16[8,128,256]{2,1,0:T(8,128)(2,1)} %bitcast.42), calls=%async_computation.2 | async-start | bytes 1048576 | tf_op jit(solution)/shard_map/all_to_all | solution.py:61
  57.7 0.0 all-gather.2.cloned.1.call-start
  57.8 0.0 copy-done.7
  57.8 0.1 reshape.83
  57.9 0.0 copy-done.8
  57.9 0.1 iota_compare_fusion
  58.0 13.4 %all-to-all-done.2 = bf16[8,128,256]{2,1,0:T(8,128)(2,1)} async-done(((bf16[8,128,256]{2,1,0:T(8,128)(2,1)}), bf16[8,128,256]{2,1,0:T(8,128)(2,1)}, u32[]{:S(2)}, u32[]{:S(2)}) %all-to-all-start.2) | async-done | bytes 524320 | tf_op jit(solution)/shard_map/all_to_all | solution.py:61
  71.4 2.2 broadcast_select_fusion.5
  73.6 3.1 %pad_maximum_fusion = bf16[6144,256]{1,0:T(8,128)(2,1)} fusion(bf16[1024,256]{1,0:T(8,128)(2,1)S(1)} %bitcast.41, bf16[4096,256]{1,0:T(8,128)(2,1)} %param.17, bf16[1024,256]{1,0:T(8,128)(2,1)} %param.16), kind=kLoop, calls=%fused_computation.6 | loop fusion | flops 9437184 | bytes 6291456 | tf_op jit(solution)/shard_map/concatenate | solution.py:14
  76.7 7.9 %gather_fusion.1 = bf16[96,128,256]{2,1,0:T(8,128)(2,1)} fusion(bf16[48,128,256]{2,1,0:T(8,128)(2,1)} %bitcast.39, s32[1024]{0:T(1024)S(1)} %pad_clamp_fusion), kind=kCustom, calls=%fused_computation.1.clone | custom fusion | bytes 12583296 | tf_op jit(solution)/shard_map/jit(_take)/gather | solution.py:16
  84.6 3.4 %broadcast_select_fusion = bf16[96,128,256]{2,1,0:T(8,128)(2,1)S(1)} fusion(bf16[96,128,256]{2,1,0:T(8,128)(2,1)} %gather_fusion.1, pred[96]{0:T(512)(128)(4,1)S(1)} %compare_and_fusion.1), kind=kLoop, calls=%fused_computation.4 | loop fusion | flops 3145728 | bytes 12583008 | tf_op jit(solution)/shard_map/jit(_take)/select_n | solution.py:16
  88.1 0.0 copy-start.2
  88.1 0.0 copy-done
  88.1 0.0 copy-start.5
  88.1 1.2 fusion.1
  89.3 0.0 copy-done.2
  89.3 0.1 bitcast_add_fusion.1
  89.5 0.0 copy-done.5
  89.5 1.2 fusion.6
  90.6 0.0 all-gather.2.cloned.1.call-update
  90.7 0.0 all-reduce.2.cloned.1.call-start
  90.7 3.2 %pad_maximum_fusion.1 = bf16[6144,256]{1,0:T(8,128)(2,1)} fusion(bf16[1024,256]{1,0:T(8,128)(2,1)} %bitcast.40, bf16[4096,256]{1,0:T(8,128)(2,1)} %param.18, bf16[1024,256]{1,0:T(8,128)(2,1)} %fusion.6), kind=kLoop, calls=%fused_computation.7 | loop fusion | flops 9437184 | bytes 6291456 | tf_op jit(solution)/shard_map/concatenate | solution.py:14
  93.9 7.9 %gather_fusion.3 = bf16[96,128,256]{2,1,0:T(8,128)(2,1)} fusion(bf16[48,128,256]{2,1,0:T(8,128)(2,1)} %bitcast.38, s32[1024]{0:T(1024)S(1)} %pad_clamp_fusion), kind=kCustom, calls=%fused_computation.3.clone | custom fusion | bytes 12583296 | tf_op jit(solution)/shard_map/jit(_take)/gather | solution.py:16
  101.9 3.4 %broadcast_select_fusion.1 = bf16[96,128,256]{2,1,0:T(8,128)(2,1)S(1)} fusion(bf16[96,128,256]{2,1,0:T(8,128)(2,1)} %gather_fusion.3, pred[96]{0:T(512)(128)(4,1)S(1)} %compare_and_fusion.1), kind=kLoop, calls=%fused_computation.5 | loop fusion | flops 3145728 | bytes 12583008 | tf_op jit(solution)/shard_map/jit(_take)/select_n | solution.py:16
  105.3 0.0 copy-start.3
  105.3 0.0 copy-start.4
  105.3 0.0 copy-start.6
  105.4 1.2 fusion
  106.6 0.0 copy-done.3
  106.6 0.1 bitcast_add_fusion
  106.7 0.0 copy-start.1
  106.7 1.0 copy-done.1
  107.7 0.0 copy-done.4
  107.7 1.0 convolution_multiply_fusion.2
  108.7 0.0 all-reduce.2.cloned.1.call-update
  108.8 2.7 %fusion.7 = bf16[1024,256]{1,0:T(8,128)(2,1)} fusion(bf16[256,256]{1,0:T(8,128)(2,1)S(1)} %copy-done.6, f32[1024,256]{1,0:T(8,128)} %copy-done.1), kind=kOutput, calls=%fused_computation.19 | convolution fusion | flops 135790592 | bytes 1703936 | tf_op jit(solution)/shard_map/dot_general | solution.py:24
  111.5 1.0 all-gather.2.cloned.1.call-done
  112.5 121.5 %all-reduce.2.cloned.1.call-done = f32[256,256]{1,0:T(8,128)} async-done(((f32[256,256]{1,0:T(8,128)}), f32[256,256]{1,0:T(8,128)}) %all-reduce.2.cloned.1.call-update) | async-done | bytes 262160 | tf_op jit(solution)/shard_map/psum | solution.py:70
  234.0 3.0 %copy.18 = bf16[4096,256]{1,0:T(8,128)(2,1)} copy(bf16[4096,256]{1,0:T(8,128)(2,1)} %all-gather.2.cloned.1.call-done) | data formatting | bytes 4194304
  237.0 1.7 copy.19
  (6 shorter events, 0.0 us)
Async XLA Ops:
  8.0 80.1 %copy-start = (bf16[8,12,128,128]{3,2,1,0:T(8,128)(2,1)S(1)}, bf16[8,12,128,128]{3,2,1,0:T(8,128)(2,1)}, u32[]{:S(2)}) copy-start(bf16[8,12,128,128]{3,2,1,0:T(8,128)(2,1)} %param.19) | copy-start | bytes 9437188
  22.0 35.8 %copy-start.7 = (s32[8,12]{1,0:T(8,128)S(1)}, s32[8,12]{1,0:T(8,128)}, u32[]{:S(2)}) copy-start(s32[8,12]{1,0:T(8,128)} %param.20) | copy-start | bytes 1156
  22.0 35.9 %copy-start.8 = (s32[1,8]{1,0:T(1,128)S(1)}, s32[1,8]{1,0:T(1,128)}, u32[]{:S(2)}) copy-start(s32[1,8]{1,0:T(1,128)} %param.22) | copy-start | bytes 100
  53.6 17.8 %all-to-all-start.2 = ((bf16[8,128,256]{2,1,0:T(8,128)(2,1)}), bf16[8,128,256]{2,1,0:T(8,128)(2,1)}, u32[]{:S(2)}, u32[]{:S(2)}) async-start(bf16[8,128,256]{2,1,0:T(8,128)(2,1)} %bitcast.42), calls=%async_computation.2 | async-start | bytes 1048576 | tf_op jit(solution)/shard_map/all_to_all | solution.py:61
  57.7 54.7 %all-gather.2.cloned.1.call-start = ((), (), s32[]{:S(2)}) async-start(), calls=%async_computation.3 | async-start | bytes 2621440 | tf_op jit(solution)/shard_map/all_gather | solution.py:62
  88.1 1.3 copy-start.2
  88.1 1.4 copy-start.5
  90.7 143.3 %all-reduce.2.cloned.1.call-start = ((), (), s32[]{:S(2)}) async-start(), calls=%async_computation.4 | async-start | bytes 524288 | tf_op jit(solution)/shard_map/psum | solution.py:70
  105.3 1.3 copy-start.3
  105.3 2.4 copy-start.4
  105.3 3.4 %copy-start.6 = (bf16[256,256]{1,0:T(8,128)(2,1)S(1)}, bf16[256,256]{1,0:T(8,128)(2,1)}, u32[]{:S(2)}) copy-start(bf16[256,256]{1,0:T(8,128)(2,1)} %param.24) | copy-start | bytes 393220
  106.7 1.0 copy-start.1
Sparse Core Ops, SparseCore 0:
  90.8 21.6 all-gather.1
Sparse Core Ops, SparseCore 1:
  108.9 125.0 all-reduce.1
where the time goes:
time: 247 us; the launch traced here: 246 us
  waiting for transfers between devices  136 us (55%)
  local copies, waits for them, and re-layouts  34.6 us (14%)
  blocking collectives  30.4 us (12%)
  other arithmetic  17.9 us (7%)
  between operations  15.7 us (6%)
  matrix products  7.36 us (3%)
  starting transfers between devices  4.23 us (2%)
    psum x1, waiting for transfers between devices, local(): grad_total = lax.psum(grad_term, ('dev', 'rep'))  121 us
    all_to_all x1, blocking collectives, local(): lax.all_to_all(serve_rows(hist_a), 'dev', split_axis=0, concat_axis=0, ti...  16.4 us
    gather x2, local copies, waits for them, and re-layouts, propagate(): jnp.take(blocks, columns.reshape(-1), axis=0)  15.8 us
    all_to_all x1, blocking collectives, local(): lax.all_to_all(wanted, 'dev', split_axis=0, concat_axis=0, tiled=True)  14 us
    all_to_all x1, waiting for transfers between devices, local(): lax.all_to_all(serve_rows(hist_b), 'dev', split_axis=0, concat_axis=0, ti...  13.4 us
    gather x2, local copies, waits for them, and re-layouts, serve_rows(): jnp.take(history, flat_rows, axis=0)  13 us
    select_n x3, other arithmetic, propagate(): jnp.take(blocks, columns.reshape(-1), axis=0)  6.85 us
    concatenate x2, other arithmetic, propagate(): jnp.concatenate([current, history, pulled.reshape(-1, feature_width)], ax...  6.33 us
  transfers between devices with their start and end apart: 3, of which 3 were waited for; matrix products, arithmetic and copies ran while one was open for 8% of the time, Pallas kernels for 0%

commit v1 on v0

--- a/solution.py
+++ b/solution.py
@@ -67,7 +67,7 @@
     grad_term = factor * lax.dot_general(
         mixed_low, grad_out, (((0,), (0,)), ((), ())), preferred_element_type=jnp.float32
     )
-    grad_total = lax.psum(grad_term, ("dev", "rep"))
+    grad_total = jnp.sum(lax.all_gather(grad_term, ("dev", "rep")), axis=0)
     return (layer_three, fresh_rows, grad_total)
 
 

time: 247 us -> 207 us (0.84)
  waiting for transfers between devices: 136 us -> 95 us
  other arithmetic: 17.9 us -> 22.6 us
    psum x1 -> x0, waiting for transfers between devices: 121 us -> none  [local(): grad_total = lax.psum(grad_term, ('dev', 'rep'))]
    all_gather x0 -> x1, waiting for transfers between devices: none -> 80.5 us  [local(): grad_total = jnp.sum(lax.all_gather(grad_term, ('dev', 'rep')), axis=0)]
    reduce_sum x0 -> x1, other arithmetic: none -> 4.63 us  [local(): grad_total = jnp.sum(lax.all_gather(grad_term, ('dev', 'rep')), axis=0)]
    unnamed x20 -> x19, local copies, waits for them, and re-layouts: 5.73 us -> 4.06 us
  transfers between devices with their start and end apart: 3 -> 3, of which waited for: 3 -> 3; matrix products, arithmetic and copies ran while one was open for 8% -> 10% of each run, Pallas kernels for 0% -> 0%
where the time goes in v1:
time: 207 us
  waiting for transfers between devices  95 us (46%)
  local copies, waits for them, and re-layouts  32.9 us (16%)
  blocking collectives  30.4 us (15%)
  other arithmetic  22.6 us (11%)
  between operations  14.2 us (7%)
  matrix products  7.34 us (4%)
  starting transfers between devices  4.23 us (2%)
    all_gather x1, waiting for transfers between devices, local(): grad_total = jnp.sum(lax.all_gather(grad_term, ('dev', 'rep')), axis=0)  80.5 us
    all_to_all x1, blocking collectives, local(): lax.all_to_all(serve_rows(hist_a), 'dev', split_axis=0, concat_axis=0, ti...  16.4 us
    gather x2, local copies, waits for them, and re-layouts, propagate(): jnp.take(blocks, columns.reshape(-1), axis=0)  15.8 us
    all_to_all x1, blocking collectives, local(): lax.all_to_all(wanted, 'dev', split_axis=0, concat_axis=0, tiled=True)  14 us
    all_to_all x1, waiting for transfers between devices, local(): lax.all_to_all(serve_rows(hist_b), 'dev', split_axis=0, concat_axis=0, ti...  13.4 us
    gather x2, local copies, waits for them, and re-layouts, serve_rows(): jnp.take(history, flat_rows, axis=0)  13 us
    select_n x3, other arithmetic, propagate(): jnp.take(blocks, columns.reshape(-1), axis=0)  6.85 us
    concatenate x2, other arithmetic, propagate(): jnp.concatenate([current, history, pulled.reshape(-1, feature_width)], ax...  6.33 us
  transfers between devices with their start and end apart: 3, of which 3 were waited for; matrix products, arithmetic and copies ran while one was open for 10% of the time, Pallas kernels for 0%

profile of v1, /device:TPU:0, one launch (start us, length us, event | category | flops | bytes accessed | tf_op | source)
XLA Modules:
  0.0 206.7 jit_solution(16577175804457388226)
XLA Ops:
  7.2 0.0 copy-start
  7.2 14.0 %all_to_all.19 = s32[8,1,128]{2,1,0:T(1,128)S(1)} all-to-all(s32[8,1,128]{2,1,0:T(1,128)} %bitcast.48), channel_id=1, replica_groups=mesh['dev'=8,'rep'=4] {'dev'}, dimensions={0} | all-to-all | bytes 8192 | tf_op jit(solution)/shard_map/all_to_all | solution.py:45
  21.2 0.0 copy-start.7
  21.2 0.0 copy-start.8
  21.2 6.5 %gather_fusion = bf16[1024,256]{1,0:T(8,128)(2,1)} fusion(bf16[4096,256]{1,0:T(8,128)(2,1)} %param.17, s32[1024]{0:T(1024)S(1)} %fusion.11), kind=kCustom, calls=%fused_computation.clone | custom fusion | bytes 1052672 | tf_op jit(solution)/shard_map/jit(_take)/gather | solution.py:52
  27.7 6.5 %gather_fusion.2 = bf16[1024,256]{1,0:T(8,128)(2,1)} fusion(bf16[4096,256]{1,0:T(8,128)(2,1)} %param.18, s32[1024]{0:T(1024)S(1)} %fusion.11), kind=kCustom, calls=%fused_computation.2.clone | custom fusion | bytes 1052672 | tf_op jit(solution)/shard_map/jit(_take)/gather | solution.py:52
  34.1 2.2 %broadcast_select_fusion.3 = (bf16[1024,256]{1,0:T(8,128)(2,1)S(1)}, bf16[1024,256]{1,0:T(8,128)(2,1)}) fusion(bf16[1024,256]{1,0:T(8,128)(2,1)} %gather_fusion, pred[1024]{0:T(1024)(128)(4,1)S(1)} %compare_and_fusion, bf16[1024,256]{1,0:T(8,128)(2,1)} %gather_fusion.2), kind=kLoop, calls=%fused_computation.26 | loop fusion | flops 524288 | bytes 2098176 | tf_op jit(solution)/shard_map/jit(_take)/select_n | solution.py:52
  36.3 16.4 %all_to_all.20 = bf16[8,128,256]{2,1,0:T(8,128)(2,1)} all-to-all(bf16[8,128,256]{2,1,0:T(8,128)(2,1)S(1)} %bitcast.45), channel_id=1, replica_groups=mesh['dev'=8,'rep'=4] {'dev'}, dimensions={0} | all-to-all | bytes 1048576 | tf_op jit(solution)/shard_map/all_to_all | solution.py:57
  52.8 4.1 %all-to-all-start.2 = ((bf16[8,128,256]{2,1,0:T(8,128)(2,1)}), bf16[8,128,256]{2,1,0:T(8,128)(2,1)}, u32[]{:S(2)}, u32[]{:S(2)}) async-start(bf16[8,128,256]{2,1,0:T(8,128)(2,1)} %bitcast.44), calls=%async_computation.2 | async-start | bytes 1048576 | tf_op jit(solution)/shard_map/all_to_all | solution.py:61
  56.9 0.0 all-gather.4.cloned.1.call-start
  57.0 0.0 copy-done.7
  57.0 0.1 reshape.83
  57.1 0.0 copy-done.8
  57.1 0.1 iota_compare_fusion
  57.2 13.4 %all-to-all-done.2 = bf16[8,128,256]{2,1,0:T(8,128)(2,1)} async-done(((bf16[8,128,256]{2,1,0:T(8,128)(2,1)}), bf16[8,128,256]{2,1,0:T(8,128)(2,1)}, u32[]{:S(2)}, u32[]{:S(2)}) %all-to-all-start.2) | async-done | bytes 524320 | tf_op jit(solution)/shard_map/all_to_all | solution.py:61
  70.6 2.2 %broadcast_select_fusion.5 = (bf16[8,128,256]{2,1,0:T(8,128)(2,1)S(1)}, bf16[8,128,256]{2,1,0:T(8,128)(2,1)}) fusion(bf16[8,128,256]{2,1,0:T(8,128)(2,1)} %all_to_all.20, pred[8,128]{1,0:T(8,128)(4,1)S(1)} %iota_compare_fusion, bf16[8,128,256]{2,1,0:T(8,128)(2,1)} %all-to-all-done.2), kind=kLoop, calls=%fused_computation.28 | loop fusion | flops 524288 | bytes 2098176 | tf_op jit(solution)/shard_map/jit(_where)/select_n | solution.py:55
  72.8 3.1 %pad_maximum_fusion = bf16[6144,256]{1,0:T(8,128)(2,1)} fusion(bf16[1024,256]{1,0:T(8,128)(2,1)S(1)} %bitcast.43, bf16[4096,256]{1,0:T(8,128)(2,1)} %param.17, bf16[1024,256]{1,0:T(8,128)(2,1)} %param.16), kind=kLoop, calls=%fused_computation.6 | loop fusion | flops 9437184 | bytes 6291456 | tf_op jit(solution)/shard_map/concatenate | solution.py:14
  75.9 7.9 %gather_fusion.1 = bf16[96,128,256]{2,1,0:T(8,128)(2,1)} fusion(bf16[48,128,256]{2,1,0:T(8,128)(2,1)} %bitcast.40, s32[1024]{0:T(1024)S(1)} %pad_clamp_fusion), kind=kCustom, calls=%fused_computation.1.clone | custom fusion | bytes 12583296 | tf_op jit(solution)/shard_map/jit(_take)/gather | solution.py:16
  83.8 3.4 %broadcast_select_fusion = bf16[96,128,256]{2,1,0:T(8,128)(2,1)S(1)} fusion(bf16[96,128,256]{2,1,0:T(8,128)(2,1)} %gather_fusion.1, pred[96]{0:T(512)(128)(4,1)S(1)} %compare_and_fusion.1), kind=kLoop, calls=%fused_computation.4 | loop fusion | flops 3145728 | bytes 12583008 | tf_op jit(solution)/shard_map/jit(_take)/select_n | solution.py:16
  87.2 0.0 copy-start.2
  87.2 0.0 copy-done
  87.2 0.0 copy-start.5
  87.3 1.2 fusion.1
  88.5 0.0 copy-done.2
  88.5 0.1 bitcast_add_fusion.1
  88.6 0.0 copy-done.5
  88.6 1.1 fusion.6
  89.8 0.0 all-gather.4.cloned.1.call-update
  89.8 0.0 all-gather.6.cloned.1.call-start
  89.9 3.2 %pad_maximum_fusion.1 = bf16[6144,256]{1,0:T(8,128)(2,1)} fusion(bf16[1024,256]{1,0:T(8,128)(2,1)} %bitcast.42, bf16[4096,256]{1,0:T(8,128)(2,1)} %param.18, bf16[1024,256]{1,0:T(8,128)(2,1)} %fusion.6), kind=kLoop, calls=%fused_computation.7 | loop fusion | flops 9437184 | bytes 6291456 | tf_op jit(solution)/shard_map/concatenate | solution.py:14
  93.1 7.9 %gather_fusion.3 = bf16[96,128,256]{2,1,0:T(8,128)(2,1)} fusion(bf16[48,128,256]{2,1,0:T(8,128)(2,1)} %bitcast.39, s32[1024]{0:T(1024)S(1)} %pad_clamp_fusion), kind=kCustom, calls=%fused_computation.3.clone | custom fusion | bytes 12583296 | tf_op jit(solution)/shard_map/jit(_take)/gather | solution.py:16
  101.0 3.4 %broadcast_select_fusion.1 = bf16[96,128,256]{2,1,0:T(8,128)(2,1)S(1)} fusion(bf16[96,128,256]{2,1,0:T(8,128)(2,1)} %gather_fusion.3, pred[96]{0:T(512)(128)(4,1)S(1)} %compare_and_fusion.1), kind=kLoop, calls=%fused_computation.5 | loop fusion | flops 3145728 | bytes 12583008 | tf_op jit(solution)/shard_map/jit(_take)/select_n | solution.py:16
  104.5 0.0 copy-start.3
  104.5 0.0 copy-start.4
  104.5 0.0 copy-start.6
  104.5 1.2 fusion
  105.7 0.0 copy-done.3
  105.7 0.1 bitcast_add_fusion
  105.9 0.0 copy-start.1
  105.9 1.0 copy-done.1
  106.8 0.0 copy-done.4
  106.8 1.0 convolution_multiply_fusion.2
  107.9 0.0 all-gather.6.cloned.1.call-update
  107.9 2.7 %fusion.7 = bf16[1024,256]{1,0:T(8,128)(2,1)} fusion(bf16[256,256]{1,0:T(8,128)(2,1)S(1)} %copy-done.6, f32[1024,256]{1,0:T(8,128)} %copy-done.1), kind=kOutput, calls=%fused_computation.19 | convolution fusion | flops 135790592 | bytes 1703936 | tf_op jit(solution)/shard_map/dot_general | solution.py:24
  110.6 1.0 all-gather.4.cloned.1.call-done
  111.6 80.5 %all-gather.6.cloned.1.call-done = f32[8192,256]{1,0:T(8,128)} async-done(((f32[256,256]{1,0:T(8,128)}), f32[8192,256]{1,0:T(8,128)}) %all-gather.6.cloned.1.call-update) | async-done | bytes 8388624 | tf_op jit(solution)/shard_map/all_gather | solution.py:70
  192.2 4.6 %reduce_sum.9 = f32[256,256]{1,0:T(8,128)} reduce(f32[32,256,256]{2,1,0:T(8,128)} %bitcast.41, f32[]{:T(128)} %constant.2.clone.1), dimensions={0}, to_apply=%region_0.3 | reduce | flops 2031616 | bytes 8650756 | tf_op jit(solution)/shard_map/reduce_sum | solution.py:70
  196.8 3.0 %copy.17 = bf16[4096,256]{1,0:T(8,128)(2,1)} copy(bf16[4096,256]{1,0:T(8,128)(2,1)} %all-gather.4.cloned.1.call-done) | data formatting | bytes 4194304
  (6 shorter events, 0.0 us)
Async XLA Ops:
  7.2 80.1 %copy-start = (bf16[8,12,128,128]{3,2,1,0:T(8,128)(2,1)S(1)}, bf16[8,12,128,128]{3,2,1,0:T(8,128)(2,1)}, u32[]{:S(2)}) copy-start(bf16[8,12,128,128]{3,2,1,0:T(8,128)(2,1)} %param.19) | copy-start | bytes 9437188
  21.2 35.8 %copy-start.7 = (s32[8,12]{1,0:T(8,128)S(1)}, s32[8,12]{1,0:T(8,128)}, u32[]{:S(2)}) copy-start(s32[8,12]{1,0:T(8,128)} %param.20) | copy-start | bytes 1156
  21.2 35.9 %copy-start.8 = (s32[1,8]{1,0:T(1,128)S(1)}, s32[1,8]{1,0:T(1,128)}, u32[]{:S(2)}) copy-start(s32[1,8]{1,0:T(1,128)} %param.22) | copy-start | bytes 100
  52.8 17.8 %all-to-all-start.2 = ((bf16[8,128,256]{2,1,0:T(8,128)(2,1)}), bf16[8,128,256]{2,1,0:T(8,128)(2,1)}, u32[]{:S(2)}, u32[]{:S(2)}) async-start(bf16[8,128,256]{2,1,0:T(8,128)(2,1)} %bitcast.44), calls=%async_computation.2 | async-start | bytes 1048576 | tf_op jit(solution)/shard_map/all_to_all | solution.py:61
  56.9 54.7 %all-gather.4.cloned.1.call-start = ((), (), s32[]{:S(2)}) async-start(), calls=%async_computation.3 | async-start | bytes 2621440 | tf_op jit(solution)/shard_map/all_gather | solution.py:62
  87.2 1.3 copy-start.2
  87.2 1.4 copy-start.5
  89.8 102.3 %all-gather.6.cloned.1.call-start = ((), (), s32[]{:S(2)}) async-start(), calls=%async_computation.4 | async-start | bytes 8650752 | tf_op jit(solution)/shard_map/all_gather | solution.py:70
  104.5 1.3 copy-start.3
  104.5 2.4 %copy-start.4 = (bf16[1024,256]{1,0:T(8,128)(2,1)S(1)}, bf16[1024,256]{1,0:T(8,128)(2,1)}, u32[]{:S(2)}) copy-start(bf16[1024,256]{1,0:T(8,128)(2,1)} %param.25) | copy-start | bytes 1572868
  104.5 3.4 %copy-start.6 = (bf16[256,256]{1,0:T(8,128)(2,1)S(1)}, bf16[256,256]{1,0:T(8,128)(2,1)}, u32[]{:S(2)}) copy-start(bf16[256,256]{1,0:T(8,128)(2,1)} %param.24) | copy-start | bytes 393220
  105.9 1.0 copy-start.1
Sparse Core Ops, SparseCore 0:
  89.9 21.6 all-gather.3
  115.1 77.0 all-gather.5
